TPU v7x, 32 devices: a whole 2x2x4 slice. The times are simulated.
32 devices in a mesh: grp: 2 (over x), ha: 16 (over z, y, core).
Axes of the slice: x: 2, y: 2, z: 4, core: 2. Of those that a mesh axis runs over, the one named last changes fastest.
Arguments:
- tokens: bfloat16 [8192, 5120], P(('grp', 'ha')), parts along dimension 0, may hold values from -6 to 6
- mod_shift: float32 [10240], P('grp'), parts along dimension 0, may hold values from -4 to 4
- mod_scale: float32 [10240], P('grp'), parts along dimension 0, may hold values from 0.25 to 1.75
- head_weight: bfloat16 [5120, 64], replicated, may hold values from -0.078125 to 0.078125
- head_bias: float32 [64], replicated, may hold values from -3 to 3
- first_kernel: bfloat16 [3, 3, 3, 16, 384], replicated, may hold values from -0.3125 to 0.3125
- first_bias: float32 [384], replicated, may hold values from -3 to 3
- norm_gain: float32 [384], replicated, may hold values from 0.25 to 1.75
- second_kernel: bfloat16 [3, 3, 3, 384, 384], replicated, may hold values from -0.0625 to 0.0625
- second_bias: float32 [384], replicated, may hold values from -2 to 2
Outputs:
- decoded: bfloat16 [4, 64, 128, 384], P(None, ('grp', 'ha')), parts along dimension 1
There are 2 independent parts, one for each index of `grp`. A program takes and returns all parts, laid end to end along the dimension named above; an argument that names none is the same for every part. Nothing has to cross between parts.
All inputs are finite; a program needn't handle non-finite values.
Results may differ from a plain program's by a relative error of at most 0.0059.
Values may be sent and summed in bfloat16 or wider, within the bound.
A program may use at most 64 MiB of HBM per device.

v0:
```python
import functools

import jax
import jax.numpy as jnp
from jax import lax
from jax.experimental import pallas as pl
from jax.experimental.pallas import tpu as pltpu
from jax.sharding import PartitionSpec as P

FRAMES = 4
VMEM_BYTES = 64_500_000
GROUP = 2
MESH = pl.DeviceIdType.MESH
F32, BF16 = jnp.float32, jnp.bfloat16


def iota(shape, dim):
    return lax.broadcasted_iota(jnp.int32, shape, dim)


def expansion(lch):
    wide = 4 * lch
    i = iota((2 * wide, 6 * 2 * wide), 0)
    o = iota((2 * wide, 6 * 2 * wide), 1)
    half, q, r, k = i // wide, i // (2 * lch) % 2, i // lch % 2, i % lch
    block, lane = o // (2 * wide), o % (2 * wide)
    ohalf, kind = block // 3, block % 3
    oq, j, ok = lane // wide, lane // lch % 4, lane % lch
    same = (half == ohalf) & (q == oq) & (k == ok)
    own = (kind == 0) & (j == r + 1)
    before = (kind == 1) & (r == 1) & (j == 0)
    after = (kind == 2) & (r == 0) & (j == 3)
    return jnp.where(same & (own | before | after), 1.0, 0.0).astype(BF16)


def kernel(
    n, lch, ch,
    tokens, shift, scale, hw, hbias, k1, b1, gain, k2, b2, out,
    tok, hwv, k1v, w1, w2, send, recv, patches, hid, z, inter, obuf,
    tok_sem, hw_sem, k1_sem, w2_sem, send_sem, recv_sem, out_sem,
):
    me = lax.axis_index("ha")
    per = n // FRAMES
    mine = lax.rem(me, per) * FRAMES
    frame = lax.div(me, per)
    cells = tok.shape[0] // FRAMES
    half = cells // 2
    width = tok.shape[1]
    wide = 4 * lch
    lanes = 2 * wide

    step = GROUP * cells
    steps = FRAMES // GROUP
    def token_copies(g):
        for i in range(g * GROUP, (g + 1) * GROUP):
            rows = pl.ds(i * cells, cells)
            yield pltpu.make_async_copy(tokens.at[rows], tok.at[rows], tok_sem.at[i])

    for copy in token_copies(0):
        copy.start()
    for g in range(2):
        pltpu.make_async_copy(hw, hwv.at[pl.ds(g * wide, wide)], hw_sem.at[g]).start()

    barrier = pltpu.get_barrier_semaphore()
    for f in range(FRAMES):
        for g in range(3):
            p = me + g - 1
            src = f * per + lax.div(jnp.clip(p, 0, n - 1), FRAMES)

            @pl.when((p >= 0) & (p < n) & (src != me))
            def _():
                pl.semaphore_signal(barrier, inc=1, device_id={"ha": src}, device_id_type=MESH)

    def targets(j):
        for g in range(3):
            to = mine + j + 1 - g
            yield g, to, (to >= 0) & (to < n)

    credits = 0
    for j in range(FRAMES):
        for g, to, ok in targets(j):
            credits = credits + jnp.where(ok & (to != me), 1, 0)

    w1[...] = jnp.zeros_like(w1)
    for g in (0, 2):
        @pl.when(me == (0 if g == 0 else n - 1))
        def _():
            for f in range(FRAMES):
                recv[f, g] = jnp.zeros((half, lanes), BF16)

    def head_rows(s):
        rows = pl.ds(s * step, step)
        acc = jnp.zeros((step, 128), F32)
        for c in range(0, width, 128):
            acc += tok[rows, c:c + 128].astype(F32)
        mean = jnp.sum(acc, axis=1, keepdims=True) * (1.0 / width)
        acc = jnp.zeros((step, 128), F32)
        for c in range(0, width, 128):
            centred = tok[rows, c:c + 128].astype(F32) - mean
            acc += centred * centred
        spread = jnp.sum(acc, axis=1, keepdims=True) * (1.0 / width)
        inv = lax.rsqrt(spread + 1e-06)
        if s == 0:
            for g in range(2):
                pltpu.make_async_copy(hw, hwv.at[pl.ds(g * wide, wide)], hw_sem.at[g]).wait()
        total = jnp.zeros((step, lanes), F32)
        for c in range(0, width, 512):
            centred = tok[rows, c:c + 512].astype(F32) - mean
            modulated = (centred * inv * scale[:, c:c + 512] + shift[:, c:c + 512]).astype(BF16)
            total += lax.dot_general(modulated, hwv[:, c:c + 512], (((1,), (1,)), ((), ())), preferred_element_type=F32)
        total = total + jnp.concatenate([hbias[...], hbias[...]], axis=1)
        low = iota((half, lanes), 1) < wide
        for a in range(GROUP):
            row = total[a * cells:(a + 1) * cells]
            send[s * GROUP + a] = jnp.where(low, row[:half], row[half:]).astype(BF16)

    for s in range(steps):
        for copy in token_copies(s):
            copy.wait()
        if s + 1 < steps:
            for copy in token_copies(s + 1):
                copy.start()
        if s == 0:
            pltpu.make_async_copy(k1, k1v, k1_sem).start()
        if s == steps - 1:
            for t in range(9):
                for dx in range(3):
                    pltpu.make_async_copy(k2.at[t * 3 + dx], w2.at[pl.ds(t * ch, ch), pl.ds(dx * ch, ch)], w2_sem.at[t * 3 + dx]).start()
        head_rows(s)
        if s == 0:
            pl.semaphore_wait(barrier, credits)
        for a in range(GROUP):
            j = s * GROUP + a
            for g, to, ok in targets(j):
                @pl.when(ok & (to != me))
                def _():
                    pltpu.make_async_remote_copy(
                        src_ref=send.at[j], dst_ref=recv.at[frame, g],
                        send_sem=send_sem.at[j, g], recv_sem=recv_sem.at[frame, g],
                        device_id={"ha": to}, device_id_type=MESH,
                    ).start()

                @pl.when(ok & (to == me))
                def _():
                    pltpu.make_async_copy(send.at[j], recv.at[frame, g], recv_sem.at[frame, g]).start()

    pltpu.make_async_copy(k1, k1v, k1_sem).wait()
    tap = 3 * lch
    for dt in range(3):
        for s in range(2):
            for r in range(2):
                for dy in range(3):
                    top = dt * 2 * lanes + (dy + s) * wide + r * lch
                    w1[top:top + tap, (2 * s + r) * ch:(2 * s + r + 1) * ch] = k1v[(dt * 3 + dy) * tap:(dt * 3 + dy + 1) * tap, :]
    spread_lanes = expansion(lch)
    place = iota((cells, lanes), 0)
    bias1, gains = [jnp.concatenate([v[i:i + 1] for i in range(ch // 128)], axis=1) for v in (b1, gain)]

    for t in range(9):
        for dx in range(3):
            pltpu.make_async_copy(k2.at[t * 3 + dx], w2.at[pl.ds(t * ch, ch), pl.ds(dx * ch, ch)], w2_sem.at[t * 3 + dx]).wait()

    edge = iota((cells, 128), 0)
    for g in range(3):
        @pl.when((me + g - 1 >= 0) & (me + g - 1 < n))
        def _():
            for f in range(FRAMES):
                pltpu.make_async_copy(send.at[0], recv.at[f, g], recv_sem.at[f, g]).wait()

    def hidden_frame(f):
        rows = recv[f].reshape(3 * half, lanes)
        opened = jnp.dot(rows, spread_lanes, preferred_element_type=F32)
        for g in range(3):
            got = opened[g * half:(g + 1) * half]
            own, before, after = [
                jnp.concatenate([got[:, kind * lanes:(kind + 1) * lanes], got[:, (3 + kind) * lanes:(4 + kind) * lanes]], axis=0)
                for kind in range(3)
            ]
            before = jnp.where(place == 0, 0.0, pltpu.roll(before, 1, 0))
            after = jnp.where(place == cells - 1, 0.0, pltpu.roll(after, cells - 1, 0))
            patches[f, :, g * lanes:(g + 1) * lanes] = (own + before + after).astype(BF16)

        first_dt = max(0, 2 - f)
        for pair in range(2):
            left = jnp.concatenate(
                [patches[f + dt - 2, :, pair * lanes:(pair + 2) * lanes] for dt in range(first_dt, 3)], axis=1)
            for s in range(2):
                y = 2 * pair + s
                first = jnp.dot(left, w1[first_dt * 2 * lanes:, 2 * s * ch:2 * (s + 1) * ch], preferred_element_type=F32)
                for r in range(2):
                    v = first[:, r * ch:(r + 1) * ch] + bias1
                    meansq = jnp.sum(v * v, axis=1, keepdims=True) * (1.0 / ch)
                    v = v * lax.rsqrt(meansq + 1e-06) * gains
                    v = 0.5 * v
                    v = v * jnp.tanh(v) + v
                    if y == 0:
                        v = jnp.where(me == 0, 0.0, v)
                    if y == 3:
                        v = jnp.where(me == n - 1, 0.0, v)
                    hid[f, y, r * cells:(r + 1) * cells, :] = v.astype(BF16)

    def decoded_frame(f):
        first_dt = max(0, 2 - f)
        left = jnp.concatenate(
            [hid[f + dt - 2, dy:dy + 2].reshape(4 * cells, ch) for dt in range(first_dt, 3) for dy in range(3)], axis=1)
        for c in range(0, 3 * ch, 256):
            e = min(c + 256, 3 * ch)
            z[f, :, c:e] = jnp.dot(left, w2[first_dt * 3 * ch:, c:e], preferred_element_type=F32)
        for y in range(2):
            def part(r, dx, c):
                top = (2 * y + r) * cells
                return z[f, top:top + cells, dx * ch + c:dx * ch + c + 128]

            for c in range(0, ch, 128):
                bias = b2[c // 128:c // 128 + 1]
                before = jnp.where(edge == 0, 0.0, pltpu.roll(part(1, 0, c), 1, 0))
                after = jnp.where(edge == cells - 1, 0.0, pltpu.roll(part(0, 2, c), cells - 1, 0))
                lane = inter.at[f, y, c // 128]
                lane[pl.ds(0, cells, stride=2), :] = before + part(0, 1, c) + part(1, 2, c) + bias
                lane[pl.ds(1, cells, stride=2), :] = part(0, 0, c) + part(1, 1, c) + after + bias
                obuf[f, y, :, c:c + 128] = lane[...].astype(BF16)
        pltpu.make_async_copy(obuf.at[f], out.at[f], out_sem.at[f]).start()

    hidden_frame(0)
    for f in range(FRAMES):
        if f + 1 < FRAMES:
            hidden_frame(f + 1)
        decoded_frame(f)

    for j in range(FRAMES):
        for g, to, ok in targets(j):
            @pl.when(ok & (to != me))
            def _():
                pltpu.make_async_remote_copy(
                    src_ref=send.at[j], dst_ref=recv.at[frame, g],
                    send_sem=send_sem.at[j, g], recv_sem=recv_sem.at[frame, g],
                    device_id={"ha": to}, device_id_type=MESH,
                ).wait_send()
    for f in range(FRAMES):
        pltpu.make_async_copy(obuf.at[f], out.at[f], out_sem.at[f]).wait()


def on_device(tokens, mod_shift, mod_scale, head_weight, head_bias, first_kernel, first_bias, norm_gain, second_kernel, second_bias):
    n = lax.axis_size("ha")
    count, width = tokens.shape
    lch, ch = first_kernel.shape[3:]
    cells = count // FRAMES
    lanes = 8 * lch
    anywhere = pl.BlockSpec(memory_space=pl.ANY)
    vmem = pl.BlockSpec(memory_space=pltpu.VMEM)
    dma = pltpu.SemaphoreType.DMA
    return pl.pallas_call(
        functools.partial(kernel, n, lch, ch),
        name="decode",
        out_shape=jax.ShapeDtypeStruct((FRAMES, 2, 2 * cells, ch), BF16),
        in_specs=[anywhere, vmem, vmem, anywhere, vmem, anywhere, vmem, vmem, anywhere, vmem],
        out_specs=anywhere,
        scratch_shapes=[
            pltpu.VMEM((count, width), BF16),
            pltpu.VMEM((lanes, width), BF16),
            pltpu.VMEM((27 * lch, ch), BF16),
            pltpu.VMEM((6 * lanes, 4 * ch), BF16),
            pltpu.VMEM((9 * ch, 3 * ch), BF16),
            pltpu.VMEM((FRAMES, cells // 2, lanes), BF16),
            pltpu.VMEM((FRAMES, 3, cells // 2, lanes), BF16),
            pltpu.VMEM((FRAMES, cells, 3 * lanes), BF16),
            pltpu.VMEM((FRAMES, 4, 2 * cells, ch), BF16),
            pltpu.VMEM((FRAMES, 4 * cells, 3 * ch), F32),
            pltpu.VMEM((FRAMES, 2, ch // 128, 2 * cells, 128), F32),
            pltpu.VMEM((FRAMES, 2, 2 * cells, ch), BF16),
            dma((FRAMES,)),
            dma((2,)),
            dma,
            dma((27,)),
            dma((FRAMES, 3)),
            dma((FRAMES, 3)),
            dma((FRAMES,)),
        ],
        compiler_params=pltpu.CompilerParams(collective_id=0, has_side_effects=True, vmem_limit_bytes=VMEM_BYTES),
    )(
        tokens, mod_shift.reshape(1, width), mod_scale.reshape(1, width), head_weight.T, head_bias.reshape(1, -1),
        first_kernel.reshape(27 * lch, ch), first_bias.reshape(-1, 128), norm_gain.reshape(-1, 128),
        second_kernel.reshape(27, ch, ch), second_bias.reshape(-1, 128),
    )


def solution(mesh):
    return jax.shard_map(
        on_device,
        mesh=mesh,
        in_specs=(P(("grp", "ha"), None), P("grp"), P("grp"), P(), P(), P(), P(), P(), P(), P()),
        out_specs=P(None, ("grp", "ha"), None, None),
        check_vma=False,
    )
```

profile of v0, /device:TPU:1, one launch (start us, length us, event | category | flops | bytes accessed | tf_op | source)
XLA Modules:
  0.0 25.4 jit_solution(13891576012222571275)
XLA Ops:
  0.0 23.3 %decode.1 = bf16[4,2,128,384]{3,2,1,0:T(8,128)(2,1)} custom-call(bf16[256,5120]{1,0:T(8,128)(2,1)} %tokens.1, f32[1,5120]{1,0:T(1,128)} %bitcast.12, f32[1,5120]{1,0:T(1,128)} %bitcast.13, bf16[64,5120]{1,0:T(8,128)(2,1)} %bitcast.10, f32[1,64]{1,0:T(1,128)} %bitcast.17, bf16[432,384]{1,0:T(8,128)(2,1)} %bitcast.11, f32[3,128]{1,0:T(4,128)} %bitcast.14, ...), custom_call_target="tpu_custom_call" | custom-call | tf_op jit(solution)/shard_map/decode/pallas_call | solution.py:252
  23.4 2.1 %copy.12 = bf16[4,2,128,384]{3,2,1,0:T(8,128)(2,1)} copy(bf16[4,2,128,384]{3,2,1,0:T(8,128)(2,1)} %decode.1) | data formatting | bytes 1572864
where the time goes:
time: 25.7 us; the launch traced here: 25.4 us
  Pallas kernels  23.3 us (91%)
  local copies, waits for them, and re-layouts  2.09 us (8%)
    pallas_call x1, Pallas kernels, on_device(): pl.pallas_call(functools.partial(kernel, n, lch, ch), name='decode', out_...  23.3 us
    unnamed x1, local copies, waits for them, and re-layouts  2.09 us

commit v1 on v0

--- a/solution.py
+++ b/solution.py
@@ -8,7 +8,7 @@
 from jax.sharding import PartitionSpec as P
 
 FRAMES = 4
-VMEM_BYTES = 64_500_000
+VMEM_BYTES = 56_000_000
 GROUP = 2
 MESH = pl.DeviceIdType.MESH
 F32, BF16 = jnp.float32, jnp.bfloat16
@@ -35,9 +35,10 @@
 
 def kernel(
     n, lch, ch,
-    tokens, shift, scale, hw, hbias, k1, b1, gain, k2, b2, out,
-    tok, hwv, k1v, w1, w2, send, recv, patches, hid, z, inter, obuf,
-    tok_sem, hw_sem, k1_sem, w2_sem, send_sem, recv_sem, out_sem,
+    tokens, shift_in, scale_in, hw, hbias_in, k1, b1_in, gain_in, k2, b2_in, obuf,
+    tok, hwv, k1v, w1, w2, send, recv, patches, hid, z, inter,
+    shift, scale, hbias, b1, gain, b2,
+    tok_sem, hw_sem, k1_sem, w2_sem, send_sem, recv_sem, small_sem,
 ):
     me = lax.axis_index("ha")
     per = n // FRAMES
@@ -56,10 +57,16 @@
             rows = pl.ds(i * cells, cells)
             yield pltpu.make_async_copy(tokens.at[rows], tok.at[rows], tok_sem.at[i])
 
+    small = [
+        pltpu.make_async_copy(src, dst, small_sem.at[i])
+        for i, (src, dst) in enumerate(zip((scale_in, shift_in, hbias_in, b1_in, gain_in, b2_in), (scale, shift, hbias, b1, gain, b2)))
+    ]
     for copy in token_copies(0):
         copy.start()
     for g in range(2):
         pltpu.make_async_copy(hw, hwv.at[pl.ds(g * wide, wide)], hw_sem.at[g]).start()
+    for copy in small:
+        copy.start()
 
     barrier = pltpu.get_barrier_semaphore()
     for f in range(FRAMES):
@@ -103,6 +110,8 @@
         if s == 0:
             for g in range(2):
                 pltpu.make_async_copy(hw, hwv.at[pl.ds(g * wide, wide)], hw_sem.at[g]).wait()
+            for copy in small:
+                copy.wait()
         total = jnp.zeros((step, lanes), F32)
         for c in range(0, width, 512):
             centred = tok[rows, c:c + 512].astype(F32) - mean
@@ -219,7 +228,6 @@
                 lane[pl.ds(0, cells, stride=2), :] = before + part(0, 1, c) + part(1, 2, c) + bias
                 lane[pl.ds(1, cells, stride=2), :] = part(0, 0, c) + part(1, 1, c) + after + bias
                 obuf[f, y, :, c:c + 128] = lane[...].astype(BF16)
-        pltpu.make_async_copy(obuf.at[f], out.at[f], out_sem.at[f]).start()
 
     hidden_frame(0)
     for f in range(FRAMES):
@@ -236,8 +244,14 @@
                     send_sem=send_sem.at[j, g], recv_sem=recv_sem.at[frame, g],
                     device_id={"ha": to}, device_id_type=MESH,
                 ).wait_send()
-    for f in range(FRAMES):
-        pltpu.make_async_copy(obuf.at[f], out.at[f], out_sem.at[f]).wait()
+
+
+def store_kernel(held, out, sem):
+    copies = [pltpu.make_async_copy(held.at[f], out.at[f], sem.at[f]) for f in range(FRAMES)]
+    for copy in copies:
+        copy.start()
+    for copy in copies:
+        copy.wait()
 
 
 def on_device(tokens, mod_shift, mod_scale, head_weight, head_bias, first_kernel, first_bias, norm_gain, second_kernel, second_bias):
@@ -249,12 +263,12 @@
     anywhere = pl.BlockSpec(memory_space=pl.ANY)
     vmem = pl.BlockSpec(memory_space=pltpu.VMEM)
     dma = pltpu.SemaphoreType.DMA
-    return pl.pallas_call(
+    held = pl.pallas_call(
         functools.partial(kernel, n, lch, ch),
         name="decode",
-        out_shape=jax.ShapeDtypeStruct((FRAMES, 2, 2 * cells, ch), BF16),
-        in_specs=[anywhere, vmem, vmem, anywhere, vmem, anywhere, vmem, vmem, anywhere, vmem],
-        out_specs=anywhere,
+        out_shape=pltpu.VMEM((FRAMES, 2, 2 * cells, ch), BF16),
+        in_specs=[anywhere] * 10,
+        out_specs=vmem,
         scratch_shapes=[
             pltpu.VMEM((count, width), BF16),
             pltpu.VMEM((lanes, width), BF16),
@@ -267,14 +281,19 @@
             pltpu.VMEM((FRAMES, 4, 2 * cells, ch), BF16),
             pltpu.VMEM((FRAMES, 4 * cells, 3 * ch), F32),
             pltpu.VMEM((FRAMES, 2, ch // 128, 2 * cells, 128), F32),
-            pltpu.VMEM((FRAMES, 2, 2 * cells, ch), BF16),
+            pltpu.VMEM((1, width), F32),
+            pltpu.VMEM((1, width), F32),
+            pltpu.VMEM((1, 4 * lch), F32),
+            pltpu.VMEM((ch // 128, 128), F32),
+            pltpu.VMEM((ch // 128, 128), F32),
+            pltpu.VMEM((ch // 128, 128), F32),
             dma((FRAMES,)),
             dma((2,)),
             dma,
             dma((27,)),
             dma((FRAMES, 3)),
             dma((FRAMES, 3)),
-            dma((FRAMES,)),
+            dma((6,)),
         ],
         compiler_params=pltpu.CompilerParams(collective_id=0, has_side_effects=True, vmem_limit_bytes=VMEM_BYTES),
     )(
@@ -282,6 +301,14 @@
         first_kernel.reshape(27 * lch, ch), first_bias.reshape(-1, 128), norm_gain.reshape(-1, 128),
         second_kernel.reshape(27, ch, ch), second_bias.reshape(-1, 128),
     )
+    return pl.pallas_call(
+        store_kernel,
+        name="store",
+        out_shape=jax.ShapeDtypeStruct(held.shape, BF16),
+        in_specs=[vmem],
+        out_specs=anywhere,
+        scratch_shapes=[dma((FRAMES,))],
+    )(pltpu.with_memory_space_constraint(held, pltpu.VMEM))
 
 
 def solution(mesh):

time: 25.7 us -> 23.3 us (0.907)
  local copies, waits for them, and re-layouts: 2.09 us -> 0 us
  Pallas kernels: 23.3 us -> 23 us
    unnamed x1 -> x0, local copies, waits for them, and re-layouts: 2.09 us -> none
    pallas_call x1, Pallas kernels: 23.3 us -> 22 us  [on_device(): pl.pallas_call(functools.partial(kernel, n, lch, ch), name='decode', out_...]
    pallas_call x0 -> x1, Pallas kernels: none -> 0.91 us  [on_device(): pl.pallas_call(store_kernel, name='store', out_shape=jax.ShapeDtypeStruct...]
where the time goes in v1:
time: 23.3 us; the launch traced here: 23.1 us
  Pallas kernels  23 us (99%)
    pallas_call x1, Pallas kernels, on_device(): pl.pallas_call(functools.partial(kernel, n, lch, ch), name='decode', out_...  22 us
    pallas_call x1, Pallas kernels, on_device(): pl.pallas_call(store_kernel, name='store', out_shape=jax.ShapeDtypeStruct...  0.91 us

profile of v1, /device:TPU:1, one launch (start us, length us, event | category | flops | bytes accessed | tf_op | source)
XLA Modules:
  0.0 23.1 jit_solution(13003937417022690950)
XLA Ops:
  0.0 22.0 %decode.1.held = bf16[4,2,128,384]{3,2,1,0:T(8,128)(2,1)S(1)} custom-call(bf16[256,5120]{1,0:T(8,128)(2,1)} %tokens.1, f32[1,5120]{1,0:T(1,128)} %bitcast.12, f32[1,5120]{1,0:T(1,128)} %bitcast.13, bf16[64,5120]{1,0:T(8,128)(2,1)} %bitcast.10, f32[1,64]{1,0:T(1,128)} %bitcast.17, bf16[432,384]{1,0:T(8,128)(2,1)} %bitcast.11, f32[3,128]{1,0:T(4,128)} %bitcast.14, ...), custom_call_target="tpu_custom_call" | custom-call | tf_op jit(solution)/shard_map/decode/pallas_call | solution.py:266
  22.1 0.9 %store.1 = bf16[4,2,128,384]{3,2,1,0:T(8,128)(2,1)} custom-call(bf16[4,2,128,384]{3,2,1,0:T(8,128)(2,1)S(1)} %decode.1.held), custom_call_target="tpu_custom_call" | custom-call | tf_op jit(solution)/shard_map/store/pallas_call | solution.py:304

commit v2 on v1

--- a/solution.py
+++ b/solution.py
@@ -10,6 +10,7 @@
 FRAMES = 4
 VMEM_BYTES = 56_000_000
 GROUP = 2
+TILE = 32
 MESH = pl.DeviceIdType.MESH
 F32, BF16 = jnp.float32, jnp.bfloat16
 
@@ -36,7 +37,7 @@
 def kernel(
     n, lch, ch,
     tokens, shift_in, scale_in, hw, hbias_in, k1, b1_in, gain_in, k2, b2_in, obuf,
-    tok, hwv, k1v, w1, w2, send, recv, patches, hid, z, inter,
+    tok, hwv, k1v, w1, w2, blank, send, recv, patches, hid, filters, fields, products, z, inter,
     shift, scale, hbias, b1, gain, b2,
     tok_sem, hw_sem, k1_sem, w2_sem, send_sem, recv_sem, small_sem,
 ):
@@ -67,6 +68,13 @@
         pltpu.make_async_copy(hw, hwv.at[pl.ds(g * wide, wide)], hw_sem.at[g]).start()
     for copy in small:
         copy.start()
+    for g in range(1, steps):
+        for copy in token_copies(g):
+            copy.start()
+
+    def kernel_copy(t):
+        taps = pl.ds((8 - t) * 3, 3)
+        return pltpu.make_async_copy(k2.at[taps], w2.at[taps], w2_sem.at[t])
 
     barrier = pltpu.get_barrier_semaphore()
     for f in range(FRAMES):
@@ -89,11 +97,12 @@
             credits = credits + jnp.where(ok & (to != me), 1, 0)
 
     w1[...] = jnp.zeros_like(w1)
+    blank[...] = jnp.zeros_like(blank)
     for g in (0, 2):
         @pl.when(me == (0 if g == 0 else n - 1))
         def _():
             for f in range(FRAMES):
-                recv[f, g] = jnp.zeros((half, lanes), BF16)
+                pltpu.make_async_copy(blank, recv.at[f, g], recv_sem.at[f, g]).start()
 
     def head_rows(s):
         rows = pl.ds(s * step, step)
@@ -126,15 +135,10 @@
     for s in range(steps):
         for copy in token_copies(s):
             copy.wait()
-        if s + 1 < steps:
-            for copy in token_copies(s + 1):
-                copy.start()
         if s == 0:
             pltpu.make_async_copy(k1, k1v, k1_sem).start()
-        if s == steps - 1:
             for t in range(9):
-                for dx in range(3):
-                    pltpu.make_async_copy(k2.at[t * 3 + dx], w2.at[pl.ds(t * ch, ch), pl.ds(dx * ch, ch)], w2_sem.at[t * 3 + dx]).start()
+                kernel_copy(t).start()
         head_rows(s)
         if s == 0:
             pl.semaphore_wait(barrier, credits)
@@ -164,76 +168,135 @@
     spread_lanes = expansion(lch)
     place = iota((cells, lanes), 0)
     bias1, gains = [jnp.concatenate([v[i:i + 1] for i in range(ch // 128)], axis=1) for v in (b1, gain)]
-
-    for t in range(9):
-        for dx in range(3):
-            pltpu.make_async_copy(k2.at[t * 3 + dx], w2.at[pl.ds(t * ch, ch), pl.ds(dx * ch, ch)], w2_sem.at[t * 3 + dx]).wait()
-
+    gains = 0.5 * gains
+
+    def both(a, b, c):
+        ends = a + c
+        return ends + b, ends - b
+
+    def transform(dt, rows, into):
+        raw = [[w2[dt * 9 + dy * 3 + dx, rows, :] for dx in range(3)] for dy in range(3)]
+        taps = [[x.astype(F32) for x in line] for line in raw]
+        for i in (0, 3):
+            for j in (0, 3):
+                filters[4 * i + j, into, :] = raw[2 * i // 3][2 * j // 3]
+        for j in (0, 3):
+            one, two = both(*[taps[dy][2 * j // 3] for dy in range(3)])
+            filters[4 + j, into, :] = one.astype(BF16)
+            filters[8 + j, into, :] = two.astype(BF16)
+        lines = [both(*taps[dy]) for dy in range(3)]
+        for j in (1, 2):
+            for i in (0, 3):
+                filters[4 * i + j, into, :] = lines[2 * i // 3][j - 1].astype(BF16)
+            one, two = both(*[lines[dy][j - 1] for dy in range(3)])
+            filters[4 + j, into, :] = one.astype(BF16)
+            filters[8 + j, into, :] = two.astype(BF16)
+
+    for dt in (2, 1, 0):
+        for t in range(6 - 3 * dt, 9 - 3 * dt):
+            kernel_copy(t).wait()
+
+        def body(r, carry):
+            transform(dt, pl.ds(pl.multiple_of(r * TILE, TILE), TILE), pl.ds(pl.multiple_of(dt * ch + r * TILE, TILE), TILE))
+            return carry
+
+        lax.fori_loop(0, ch // TILE, body, 0)
     edge = iota((cells, 128), 0)
-    for g in range(3):
-        @pl.when((me + g - 1 >= 0) & (me + g - 1 < n))
-        def _():
-            for f in range(FRAMES):
-                pltpu.make_async_copy(send.at[0], recv.at[f, g], recv_sem.at[f, g]).wait()
-
-    def hidden_frame(f):
-        rows = recv[f].reshape(3 * half, lanes)
+
+    def arrive(pair):
+        for f in (2 * pair, 2 * pair + 1):
+            for g in range(3):
+                pltpu.make_async_copy(blank, recv.at[f, g], recv_sem.at[f, g]).wait()
+
+    def hidden_pair(pair):
+        frames = (2 * pair, 2 * pair + 1)
+        rows = jnp.concatenate([recv[f].reshape(3 * half, lanes) for f in frames], axis=0)
         opened = jnp.dot(rows, spread_lanes, preferred_element_type=F32)
-        for g in range(3):
-            got = opened[g * half:(g + 1) * half]
-            own, before, after = [
-                jnp.concatenate([got[:, kind * lanes:(kind + 1) * lanes], got[:, (3 + kind) * lanes:(4 + kind) * lanes]], axis=0)
-                for kind in range(3)
-            ]
-            before = jnp.where(place == 0, 0.0, pltpu.roll(before, 1, 0))
-            after = jnp.where(place == cells - 1, 0.0, pltpu.roll(after, cells - 1, 0))
-            patches[f, :, g * lanes:(g + 1) * lanes] = (own + before + after).astype(BF16)
-
-        first_dt = max(0, 2 - f)
-        for pair in range(2):
-            left = jnp.concatenate(
-                [patches[f + dt - 2, :, pair * lanes:(pair + 2) * lanes] for dt in range(first_dt, 3)], axis=1)
-            for s in range(2):
-                y = 2 * pair + s
-                first = jnp.dot(left, w1[first_dt * 2 * lanes:, 2 * s * ch:2 * (s + 1) * ch], preferred_element_type=F32)
-                for r in range(2):
-                    v = first[:, r * ch:(r + 1) * ch] + bias1
-                    meansq = jnp.sum(v * v, axis=1, keepdims=True) * (1.0 / ch)
-                    v = v * lax.rsqrt(meansq + 1e-06) * gains
-                    v = 0.5 * v
-                    v = v * jnp.tanh(v) + v
-                    if y == 0:
-                        v = jnp.where(me == 0, 0.0, v)
-                    if y == 3:
-                        v = jnp.where(me == n - 1, 0.0, v)
-                    hid[f, y, r * cells:(r + 1) * cells, :] = v.astype(BF16)
-
-    def decoded_frame(f):
-        first_dt = max(0, 2 - f)
-        left = jnp.concatenate(
-            [hid[f + dt - 2, dy:dy + 2].reshape(4 * cells, ch) for dt in range(first_dt, 3) for dy in range(3)], axis=1)
-        for c in range(0, 3 * ch, 256):
-            e = min(c + 256, 3 * ch)
-            z[f, :, c:e] = jnp.dot(left, w2[first_dt * 3 * ch:, c:e], preferred_element_type=F32)
-        for y in range(2):
-            def part(r, dx, c):
-                top = (2 * y + r) * cells
-                return z[f, top:top + cells, dx * ch + c:dx * ch + c + 128]
-
+        for at, f in enumerate(frames):
+            for g in range(3):
+                got = opened[(3 * at + g) * half:(3 * at + g + 1) * half]
+                own, before, after = [
+                    jnp.concatenate([got[:, kind * lanes:(kind + 1) * lanes], got[:, (3 + kind) * lanes:(4 + kind) * lanes]], axis=0)
+                    for kind in range(3)
+                ]
+                before = jnp.where(place == 0, 0.0, pltpu.roll(before, 1, 0))
+                after = jnp.where(place == cells - 1, 0.0, pltpu.roll(after, cells - 1, 0))
+                patches[f, :, g * lanes:(g + 1) * lanes] = (own + before + after).astype(BF16)
+
+        first_dt = max(0, 1 - 2 * pair)
+        empty = jnp.zeros((cells, 2 * lanes), BF16)
+        left = jnp.concatenate([
+            jnp.concatenate(
+                [patches[f + dt - 2, :, p * lanes:(p + 2) * lanes] if f + dt >= 2 else empty for dt in range(first_dt, 3)], axis=1)
+            for f in frames for p in range(2)], axis=0)
+        for s in range(2):
+            first = jnp.dot(left, w1[first_dt * 2 * lanes:, 2 * s * ch:2 * (s + 1) * ch], preferred_element_type=F32)
+            for at, f in enumerate(frames):
+                for p in range(2):
+                    y = 2 * p + s
+                    top = (2 * at + p) * cells
+                    for r in range(2):
+                        v = first[top:top + cells, r * ch:(r + 1) * ch] + bias1
+                        meansq = jnp.sum(v * v, axis=1, keepdims=True) * (1.0 / ch)
+                        inv = lax.rsqrt(meansq + 1e-06)
+                        if y == 0:
+                            inv = jnp.where(me == 0, 0.0, inv)
+                        if y == 3:
+                            inv = jnp.where(me == n - 1, 0.0, inv)
+                        v = v * inv * gains
+                        v = v * jnp.tanh(v) + v
+                        hid[f, y, r] = v.astype(BF16)
+        for f in frames:
             for c in range(0, ch, 128):
-                bias = b2[c // 128:c // 128 + 1]
-                before = jnp.where(edge == 0, 0.0, pltpu.roll(part(1, 0, c), 1, 0))
-                after = jnp.where(edge == cells - 1, 0.0, pltpu.roll(part(0, 2, c), cells - 1, 0))
-                lane = inter.at[f, y, c // 128]
-                lane[pl.ds(0, cells, stride=2), :] = before + part(0, 1, c) + part(1, 2, c) + bias
-                lane[pl.ds(1, cells, stride=2), :] = part(0, 0, c) + part(1, 1, c) + after + bias
-                obuf[f, y, :, c:c + 128] = lane[...].astype(BF16)
-
-    hidden_frame(0)
-    for f in range(FRAMES):
-        if f + 1 < FRAMES:
-            hidden_frame(f + 1)
-        decoded_frame(f)
+                def row(y, r):
+                    return hid[f, y, r, :, c:c + 128].astype(F32)
+
+                for i, (one, two) in enumerate(((0, 2), (1, 2), (2, 1), (1, 3))):
+                    even, odd = [row(one, r) + row(two, r) if i == 1 else row(one, r) - row(two, r) for r in range(2)]
+                    ahead = jnp.where(edge == 0, 0.0, pltpu.roll(odd, 1, 0))
+                    behind = jnp.where(edge == cells - 1, 0.0, pltpu.roll(even, cells - 1, 0))
+                    for j, value in enumerate((ahead - odd, even + odd, odd - even, even - behind)):
+                        fields[4 * i + j, f, :, c:c + 128] = value.astype(BF16)
+
+    def decoded_pair(pair):
+        frames = (2 * pair, 2 * pair + 1)
+        first_dt = max(0, 1 - 2 * pair)
+        empty = jnp.zeros((cells, ch), BF16)
+        for j in range(4):
+            for i in range(4):
+                k = 4 * i + j
+                left = jnp.concatenate([
+                    jnp.concatenate([fields[k, f + dt - 2] if f + dt >= 2 else empty for dt in range(first_dt, 3)], axis=1)
+                    for f in frames], axis=0)
+                products[j % 2, i] = jnp.dot(left, filters[k, first_dt * ch:, :], preferred_element_type=F32)
+            u = [products[j % 2, i] for i in range(4)]
+            for y, value in enumerate((u[0] + 0.5 * (u[1] + u[2]), 0.5 * (u[1] - u[2]) - u[3])):
+                if j in (1, 2):
+                    value = 0.5 * value
+                if j == 0:
+                    z[pair, y, 0] = value
+                if j == 1:
+                    z[pair, y, 0] += value
+                    z[pair, y, 1] = value
+                if j == 2:
+                    z[pair, y, 0] += value
+                    z[pair, y, 1] -= value
+                if j == 3:
+                    z[pair, y, 1] -= value
+        for at, f in enumerate(frames):
+            top = at * cells
+            for y in range(2):
+                for c in range(0, ch, 128):
+                    bias = b2[c // 128:c // 128 + 1]
+                    lane = inter.at[f, y, c // 128]
+                    for r in range(2):
+                        lane[pl.ds(r, cells, stride=2), :] = z[pair, y, r, top:top + cells, c:c + 128] + bias
+                    obuf[f, y, :, c:c + 128] = lane[...].astype(BF16)
+
+    for pair in range(FRAMES // 2):
+        arrive(pair)
+        hidden_pair(pair)
+        decoded_pair(pair)
 
     for j in range(FRAMES):
         for g, to, ok in targets(j):
@@ -274,12 +337,16 @@
             pltpu.VMEM((lanes, width), BF16),
             pltpu.VMEM((27 * lch, ch), BF16),
             pltpu.VMEM((6 * lanes, 4 * ch), BF16),
-            pltpu.VMEM((9 * ch, 3 * ch), BF16),
+            pltpu.VMEM((27, ch, ch), BF16),
+            pltpu.VMEM((cells // 2, lanes), BF16),
             pltpu.VMEM((FRAMES, cells // 2, lanes), BF16),
             pltpu.VMEM((FRAMES, 3, cells // 2, lanes), BF16),
             pltpu.VMEM((FRAMES, cells, 3 * lanes), BF16),
-            pltpu.VMEM((FRAMES, 4, 2 * cells, ch), BF16),
-            pltpu.VMEM((FRAMES, 4 * cells, 3 * ch), F32),
+            pltpu.VMEM((FRAMES, 4, 2, cells, ch), BF16),
+            pltpu.VMEM((16, 3 * ch, ch), BF16),
+            pltpu.VMEM((16, FRAMES, cells, ch), BF16),
+            pltpu.VMEM((2, 4, 2 * cells, ch), F32),
+            pltpu.VMEM((FRAMES // 2, 2, 2, 2 * cells, ch), F32),
             pltpu.VMEM((FRAMES, 2, ch // 128, 2 * cells, 128), F32),
             pltpu.VMEM((1, width), F32),
             pltpu.VMEM((1, width), F32),
@@ -290,7 +357,7 @@
             dma((FRAMES,)),
             dma((2,)),
             dma,
-            dma((27,)),
+            dma((9,)),
             dma((FRAMES, 3)),
             dma((FRAMES, 3)),
             dma((6,)),

time: 23.3 us -> 18.7 us (0.80)
  Pallas kernels: 23 us -> 18.5 us
    pallas_call x1, Pallas kernels: 22 us -> 17.6 us  [on_device(): pl.pallas_call(functools.partial(kernel, n, lch, ch), name='decode', out_...]
where the time goes in v2:
time: 18.7 us; the launch traced here: 18.5 us
  Pallas kernels  18.5 us (99%)
    pallas_call x1, Pallas kernels, on_device(): pl.pallas_call(functools.partial(kernel, n, lch, ch), name='decode', out_...  17.6 us
    pallas_call x1, Pallas kernels, on_device(): pl.pallas_call(store_kernel, name='store', out_shape=jax.ShapeDtypeStruct...  0.91 us

profile of v2, /device:TPU:1, one launch (start us, length us, event | category | flops | bytes accessed | tf_op | source)
XLA Modules:
  0.0 18.5 jit_solution(8855546663890306501)
XLA Ops:
  0.0 17.6 %decode.1.held = bf16[4,2,128,384]{3,2,1,0:T(8,128)(2,1)S(1)} custom-call(bf16[256,5120]{1,0:T(8,128)(2,1)} %tokens.1, f32[1,5120]{1,0:T(1,128)} %bitcast.12, f32[1,5120]{1,0:T(1,128)} %bitcast.13, bf16[64,5120]{1,0:T(8,128)(2,1)} %bitcast.10, f32[1,64]{1,0:T(1,128)} %bitcast.17, bf16[432,384]{1,0:T(8,128)(2,1)} %bitcast.11, f32[3,128]{1,0:T(4,128)} %bitcast.14, ...), custom_call_target="tpu_custom_call" | custom-call | tf_op jit(solution)/shard_map/decode/pallas_call | solution.py:329
  17.6 0.9 %store.1 = bf16[4,2,128,384]{3,2,1,0:T(8,128)(2,1)} custom-call(bf16[4,2,128,384]{3,2,1,0:T(8,128)(2,1)S(1)} %decode.1.held), custom_call_target="tpu_custom_call" | custom-call | tf_op jit(solution)/shard_map/store/pallas_call | solution.py:371

commit v3 on v2

--- a/solution.py
+++ b/solution.py
@@ -11,6 +11,7 @@
 VMEM_BYTES = 56_000_000
 GROUP = 2
 TILE = 32
+DIRECT = 2
 MESH = pl.DeviceIdType.MESH
 F32, BF16 = jnp.float32, jnp.bfloat16
 
@@ -37,9 +38,9 @@
 def kernel(
     n, lch, ch,
     tokens, shift_in, scale_in, hw, hbias_in, k1, b1_in, gain_in, k2, b2_in, obuf,
-    tok, hwv, k1v, w1, w2, blank, send, recv, patches, hid, filters, fields, products, z, inter,
+    tok, offsets, hwv, k1v, w1, w2, blank, send, recv, patches, hid, filters, fields, products, z, inter,
     shift, scale, hbias, b1, gain, b2,
-    tok_sem, hw_sem, k1_sem, w2_sem, send_sem, recv_sem, small_sem,
+    tok_sem, hw_sem, k1_sem, w2_sem, send_sem, recv_sem, small_sem, swap_sem,
 ):
     me = lax.axis_index("ha")
     per = n // FRAMES
@@ -77,9 +78,11 @@
         return pltpu.make_async_copy(k2.at[taps], w2.at[taps], w2_sem.at[t])
 
     barrier = pltpu.get_barrier_semaphore()
+    twin = me + 1 - 2 * lax.rem(me, 2)
+    across = 2 * lax.rem(me, 2)
+    pl.semaphore_signal(barrier, inc=1, device_id={"ha": twin}, device_id_type=MESH)
     for f in range(FRAMES):
-        for g in range(3):
-            p = me + g - 1
+        for p in (me, me - 1 + across) + ((twin,) if f >= DIRECT else ()):
             src = f * per + lax.div(jnp.clip(p, 0, n - 1), FRAMES)
 
             @pl.when((p >= 0) & (p < n) & (src != me))
@@ -87,11 +90,25 @@
                 pl.semaphore_signal(barrier, inc=1, device_id={"ha": src}, device_id_type=MESH)
 
     def targets(j):
-        for g in range(3):
+        for g in (1, 2 if j % 2 == 0 else 0):
             to = mine + j + 1 - g
             yield g, to, (to >= 0) & (to < n)
-
-    credits = 0
+        g = 0 if j % 2 == 0 else 2
+        yield g, mine + j + 1 - g, frame >= DIRECT
+
+    def swap(f):
+        return pltpu.make_async_remote_copy(
+            src_ref=recv.at[f, 1], dst_ref=recv.at[f, across],
+            send_sem=swap_sem.at[f], recv_sem=recv_sem.at[f, across],
+            device_id={"ha": twin}, device_id_type=MESH,
+        )
+
+    def forward(frames):
+        for f in frames:
+            pltpu.make_async_copy(blank, recv.at[f, 1], recv_sem.at[f, 1]).wait()
+            swap(f).start()
+
+    credits = 1
     for j in range(FRAMES):
         for g, to, ok in targets(j):
             credits = credits + jnp.where(ok & (to != me), 1, 0)
@@ -113,6 +130,7 @@
         acc = jnp.zeros((step, 128), F32)
         for c in range(0, width, 128):
             centred = tok[rows, c:c + 128].astype(F32) - mean
+            offsets[:, c:c + 128] = centred
             acc += centred * centred
         spread = jnp.sum(acc, axis=1, keepdims=True) * (1.0 / width)
         inv = lax.rsqrt(spread + 1e-06)
@@ -123,8 +141,7 @@
                 copy.wait()
         total = jnp.zeros((step, lanes), F32)
         for c in range(0, width, 512):
-            centred = tok[rows, c:c + 512].astype(F32) - mean
-            modulated = (centred * inv * scale[:, c:c + 512] + shift[:, c:c + 512]).astype(BF16)
+            modulated = (offsets[:, c:c + 512] * inv * scale[:, c:c + 512] + shift[:, c:c + 512]).astype(BF16)
             total += lax.dot_general(modulated, hwv[:, c:c + 512], (((1,), (1,)), ((), ())), preferred_element_type=F32)
         total = total + jnp.concatenate([hbias[...], hbias[...]], axis=1)
         low = iota((half, lanes), 1) < wide
@@ -142,9 +159,9 @@
         head_rows(s)
         if s == 0:
             pl.semaphore_wait(barrier, credits)
-        for a in range(GROUP):
-            j = s * GROUP + a
-            for g, to, ok in targets(j):
+        for k in range(3 * GROUP):
+            j = s * GROUP + k % GROUP
+            for g, to, ok in list(targets(j))[k // GROUP:k // GROUP + 1]:
                 @pl.when(ok & (to != me))
                 def _():
                     pltpu.make_async_remote_copy(
@@ -193,6 +210,8 @@
             filters[8 + j, into, :] = two.astype(BF16)
 
     for dt in (2, 1, 0):
+        if dt == 0:
+            forward((0, 1))
         for t in range(6 - 3 * dt, 9 - 3 * dt):
             kernel_copy(t).wait()
 
@@ -205,7 +224,7 @@
 
     def arrive(pair):
         for f in (2 * pair, 2 * pair + 1):
-            for g in range(3):
+            for g in (0, 2) if f < DIRECT else range(3):
                 pltpu.make_async_copy(blank, recv.at[f, g], recv_sem.at[f, g]).wait()
 
     def hidden_pair(pair):
@@ -307,6 +326,8 @@
                     send_sem=send_sem.at[j, g], recv_sem=recv_sem.at[frame, g],
                     device_id={"ha": to}, device_id_type=MESH,
                 ).wait_send()
+    for f in range(DIRECT):
+        swap(f).wait_send()
 
 
 def store_kernel(held, out, sem):
@@ -334,6 +355,7 @@
         out_specs=vmem,
         scratch_shapes=[
             pltpu.VMEM((count, width), BF16),
+            pltpu.VMEM((GROUP * cells, width), F32),
             pltpu.VMEM((lanes, width), BF16),
             pltpu.VMEM((27 * lch, ch), BF16),
             pltpu.VMEM((6 * lanes, 4 * ch), BF16),
@@ -361,6 +383,7 @@
             dma((FRAMES, 3)),
             dma((FRAMES, 3)),
             dma((6,)),
+            dma((DIRECT,)),
         ],
         compiler_params=pltpu.CompilerParams(collective_id=0, has_side_effects=True, vmem_limit_bytes=VMEM_BYTES),
     )(

time: 18.7 us -> 18.3 us (0.979)
  Pallas kernels: 18.5 us -> 18.1 us
    pallas_call x1, Pallas kernels: 17.6 us -> 17.2 us  [on_device(): pl.pallas_call(functools.partial(kernel, n, lch, ch), name='decode', out_...]
where the time goes in v3:
time: 18.3 us; the launch traced here: 18.1 us
  Pallas kernels  18.1 us (99%)
    pallas_call x1, Pallas kernels, on_device(): pl.pallas_call(functools.partial(kernel, n, lch, ch), name='decode', out_...  17.2 us
    pallas_call x1, Pallas kernels, on_device(): pl.pallas_call(store_kernel, name='store', out_shape=jax.ShapeDtypeStruct...  0.91 us

profile of v3, /device:TPU:1, one launch (start us, length us, event | category | flops | bytes accessed | tf_op | source)
XLA Modules:
  0.0 18.1 jit_solution(16348600044216041339)
XLA Ops:
  0.0 17.2 %decode.1.held = bf16[4,2,128,384]{3,2,1,0:T(8,128)(2,1)S(1)} custom-call(bf16[256,5120]{1,0:T(8,128)(2,1)} %tokens.1, f32[1,5120]{1,0:T(1,128)} %bitcast.12, f32[1,5120]{1,0:T(1,128)} %bitcast.13, bf16[64,5120]{1,0:T(8,128)(2,1)} %bitcast.10, f32[1,64]{1,0:T(1,128)} %bitcast.17, bf16[432,384]{1,0:T(8,128)(2,1)} %bitcast.11, f32[3,128]{1,0:T(4,128)} %bitcast.14, ...), custom_call_target="tpu_custom_call" | custom-call | tf_op jit(solution)/shard_map/decode/pallas_call | solution.py:350
  17.2 0.9 %store.1 = bf16[4,2,128,384]{3,2,1,0:T(8,128)(2,1)} custom-call(bf16[4,2,128,384]{3,2,1,0:T(8,128)(2,1)S(1)} %decode.1.held), custom_call_target="tpu_custom_call" | custom-call | tf_op jit(solution)/shard_map/store/pallas_call | solution.py:394
